TPU v7x, 32 devices: a whole 2x2x4 slice. The times are simulated.
32 devices in a mesh: band: 8 (over z, x), patch: 4 (over y, core).
Axes of the slice: x: 2, y: 2, z: 4, core: 2. Of those that a mesh axis runs over, the one named last changes fastest.
Arguments:
- latents: bfloat16 [8, 10240, 512], P('band', 'patch'), may hold values from -6 to 6
- owners: int32 [16], replicated, may hold values from 0 to 3, as said below
- block_rows: int32 [16, 128], replicated, may hold values from 0 to 2559
- interp_weights: bfloat16 [16, 1024, 128], P('band', 'patch'), may hold values from -0.5 to 0.5
- w_first: bfloat16 [8, 512, 512], P('band'), may hold values from -0.25 to 0.25
- b_first: float32 [8, 512], P('band'), may hold values from -3 to 3
- w_second: bfloat16 [8, 512, 512], P('band'), may hold values from -0.25 to 0.25
- b_second: float32 [8, 512], P('band'), may hold values from -4 to 4
- gain: float32 [8, 512], P('band'), may hold values from 0.1 to 1.9
- w_out: bfloat16 [8, 12, 512], P('band'), may hold values from -0.25 to 0.25
- b_out: float32 [8, 12], P('band'), may hold values from -4 to 4
Outputs:
- grid_fields: float32 [8, 12, 16384], P('band', None, 'patch')
Inputs may be any that keep to these rules, and one draw needn't show every extreme that they name: `owners`: no patch owns more than 8 tiles, and one patch owns exactly 8.
All inputs are finite; a program needn't handle non-finite values.
Results may differ from a plain program's by a relative error of at most 0.003.
Values may be sent and summed in bfloat16 or wider, within the bound.
A program may use at most 64 MiB of HBM per device.

v0:
```python
import jax
import jax.numpy as jnp
from jax import lax
from jax.sharding import PartitionSpec as P


def decode_rows(interp, w_first, b_first, w_second, b_second, gain, w_out, b_out):
    hidden = jax.nn.silu(
        jnp.dot(interp, w_first, preferred_element_type=jnp.float32) + b_first
    ).astype(jnp.bfloat16)
    second = jnp.dot(hidden, w_second, preferred_element_type=jnp.float32) + b_second
    mean_value = jnp.mean(second, axis=-1, keepdims=True)
    centred = second - mean_value
    variance = jnp.mean(centred * centred, axis=-1, keepdims=True)
    normed = (centred * lax.rsqrt(variance + 1e-05) * gain).astype(jnp.bfloat16)
    result = lax.dot_general(
        w_out, normed, (((1,), (1,)), ((), ())), preferred_element_type=jnp.float32
    )
    return result + b_out[:, None]


def body(
    latents,
    owners,
    block_rows,
    interp_weights,
    w_first,
    b_first,
    w_second,
    b_second,
    gain,
    w_out,
    b_out,
):
    tile_count = owners.shape[0]
    cell_count = interp_weights.shape[1]
    channels = w_out.shape[1]
    local_latents = latents[0]
    width = local_latents.shape[1]
    weights_all = lax.all_gather(interp_weights, "band", axis=0, tiled=True)

    def decode_tile(tile_index, block):
        tile_weights = lax.dynamic_index_in_dim(weights_all, tile_index, 0, keepdims=False)
        interp = jnp.dot(tile_weights, block, preferred_element_type=jnp.float32).astype(
            jnp.bfloat16
        )
        return decode_rows(
            interp, w_first[0], b_first[0], w_second[0], b_second[0], gain[0], w_out[0], b_out[0]
        )

    empty = jnp.zeros((channels, tile_count, cell_count), jnp.float32)
    my_index = lax.axis_index("patch")
    own_tiles = jnp.take(local_latents, block_rows.reshape(-1), axis=0).reshape(
        tile_count, -1, width
    )
    mine = (owners == my_index)[:, None, None]
    filled = jnp.where(mine, own_tiles.astype(jnp.float32), jnp.float32(0.0))
    all_blocks = lax.psum(filled.astype(jnp.bfloat16), "patch")

    def visit_summed(turn_index, buffer):
        tile_index = turn_index % tile_count
        block = lax.dynamic_index_in_dim(all_blocks, tile_index, 0, keepdims=False)
        result = decode_tile(tile_index, block)
        return lax.dynamic_update_index_in_dim(buffer, result, tile_index, 1)

    decoded = lax.fori_loop(0, tile_count, visit_summed, empty)
    regrid = lax.all_to_all(decoded, "patch", split_axis=1, concat_axis=2, tiled=True)
    return regrid.reshape(channels, -1)[None]


def solution(mesh):
    return jax.shard_map(
        body,
        mesh=mesh,
        in_specs=(
            P("band", "patch", None),
            P(),
            P(),
            P("band", "patch", None),
            P("band", None, None),
            P("band", None),
            P("band", None, None),
            P("band", None),
            P("band", None),
            P("band", None, None),
            P("band", None),
        ),
        out_specs=P("band", None, "patch"),
        check_vma=False,
    )
```

profile of v0, /device:TPU:0, one launch (start us, length us, event | category | flops | bytes accessed | tf_op | source)
XLA Modules:
  0.0 144.4 jit_solution(14935995324864705536)
XLA Ops:
  7.4 0.9 compare_and_fusion
  8.2 0.7 compare_select_fusion
  9.1 9.2 %gather_fusion = bf16[2048,512]{1,0:T(8,128)(2,1)} fusion(bf16[2560,512]{1,0:T(8,128)(2,1)S(1)} %bitcast.62, s32[2048]{0:T(1024)S(1)} %broadcast_clamp_fusion), kind=kCustom, calls=%fused_computation | custom fusion | bytes 4202496 | tf_op jit(solution)/shard_map/jit(_take)/gather | solution.py:53
  18.3 2.9 %select_convert_fusion = bf16[16,128,512]{2,1,0:T(8,128)(2,1)} fusion(bf16[16,128,512]{2,1,0:T(8,128)(2,1)} %bitcast.63, pred[16]{0:T(512)(128)(4,1)S(1)} %broadcast_compare_fusion, pred[16,128]{1,0:T(8,128)(4,1)S(1)} %compare_and_fusion), kind=kLoop, calls=%fused_computation.23 | loop fusion | flops 4194304 | bytes 4196368 | tf_op jit(solution)/shard_map/convert_element_type | solution.py:58
  21.3 0.5 all-gather.2.cloned.1.call-update
  21.9 53.7 %all-reduce.2.cloned.1.call-done = bf16[16,128,512]{2,1,0:T(8,128)(2,1)} async-done(((bf16[16,128,512]{2,1,0:T(8,128)(2,1)}), bf16[16,128,512]{2,1,0:T(8,128)(2,1)}) %all-reduce.2.cloned.1.call-update) | async-done | bytes 2097168 | tf_op jit(solution)/shard_map/psum | solution.py:58
  75.6 0.7 broadcast_in_dim.43
  76.3 50.2 %while.15 = (s32[]{:T(128)}, f32[12,16,256]{2,0,1:T(8,128)}, bf16[16,256,128]{2,1,0:T(8,128)(2,1)}, bf16[16,128,512]{2,1,0:T(8,128)(2,1)}, bf16[1,512,512]{2,1,0...) while((s32[]{:T(128)}, f32[12,16,256]{2,0,1:T(8,128)}, ...), condition=%wide.region_4.5_spmd, body=%wide.region_1.4_spmd.sunk | while | flops 307236096 | bytes 3387677 | solution.py:66
  76.3 1.7 %multiply_convert_fusion.6 = bf16[256,512]{1,0:T(8,128)(2,1)S(1)} fusion(bf16[1,512,512]{2,1,0:T(8,128)(2,1)} %get-tuple-element.400, f32[512]{0:T(512)S(1)} %bitcast.71, bf16[16,128,512]{2,1,0:T(8,128)(2,1)} %get-tuple-element.399, s32[]{:T(128)S(6)} %select_n.74, bf16[16,256,128]{2,1,0:T(8,128)(2,1)} %get-tuple-element.398), kind=kOutput, calls=%fused_computation.11.clone.1 | convolution fusion | flops 168689664 | bytes 986112 | tf_op jit(solution)/shard_map/while/body/eval_jaxpr/dot_general | solution.py:9
  78.0 0.4 fusion.34
  78.4 0.2 multiply_reduce_fusion.2
  78.6 0.9 fusion.35
  79.5 1.6 %multiply_convert_fusion.6 = bf16[256,512]{1,0:T(8,128)(2,1)S(1)} fusion(bf16[1,512,512]{2,1,0:T(8,128)(2,1)} %get-tuple-element.400, f32[512]{0:T(512)S(1)} %bitcast.71, bf16[16,128,512]{2,1,0:T(8,128)(2,1)} %get-tuple-element.399, s32[]{:T(128)S(6)} %select_n.74, bf16[16,256,128]{2,1,0:T(8,128)(2,1)} %get-tuple-element.398), kind=kOutput, calls=%fused_computation.11.clone.1 | convolution fusion | flops 168689664 | bytes 986112 | tf_op jit(solution)/shard_map/while/body/eval_jaxpr/dot_general | solution.py:9
  81.1 0.4 fusion.34
  81.5 0.2 multiply_reduce_fusion.2
  81.7 0.9 fusion.35
  82.6 1.6 %multiply_convert_fusion.6 = bf16[256,512]{1,0:T(8,128)(2,1)S(1)} fusion(bf16[1,512,512]{2,1,0:T(8,128)(2,1)} %get-tuple-element.400, f32[512]{0:T(512)S(1)} %bitcast.71, bf16[16,128,512]{2,1,0:T(8,128)(2,1)} %get-tuple-element.399, s32[]{:T(128)S(6)} %select_n.74, bf16[16,256,128]{2,1,0:T(8,128)(2,1)} %get-tuple-element.398), kind=kOutput, calls=%fused_computation.11.clone.1 | convolution fusion | flops 168689664 | bytes 986112 | tf_op jit(solution)/shard_map/while/body/eval_jaxpr/dot_general | solution.py:9
  84.2 0.4 fusion.34
  84.6 0.2 multiply_reduce_fusion.2
  84.9 0.9 fusion.35
  85.7 1.6 %multiply_convert_fusion.6 = bf16[256,512]{1,0:T(8,128)(2,1)S(1)} fusion(bf16[1,512,512]{2,1,0:T(8,128)(2,1)} %get-tuple-element.400, f32[512]{0:T(512)S(1)} %bitcast.71, bf16[16,128,512]{2,1,0:T(8,128)(2,1)} %get-tuple-element.399, s32[]{:T(128)S(6)} %select_n.74, bf16[16,256,128]{2,1,0:T(8,128)(2,1)} %get-tuple-element.398), kind=kOutput, calls=%fused_computation.11.clone.1 | convolution fusion | flops 168689664 | bytes 986112 | tf_op jit(solution)/shard_map/while/body/eval_jaxpr/dot_general | solution.py:9
  87.4 0.4 fusion.34
  87.8 0.2 multiply_reduce_fusion.2
  88.0 0.9 fusion.35
  88.9 1.6 %multiply_convert_fusion.6 = bf16[256,512]{1,0:T(8,128)(2,1)S(1)} fusion(bf16[1,512,512]{2,1,0:T(8,128)(2,1)} %get-tuple-element.400, f32[512]{0:T(512)S(1)} %bitcast.71, bf16[16,128,512]{2,1,0:T(8,128)(2,1)} %get-tuple-element.399, s32[]{:T(128)S(6)} %select_n.74, bf16[16,256,128]{2,1,0:T(8,128)(2,1)} %get-tuple-element.398), kind=kOutput, calls=%fused_computation.11.clone.1 | convolution fusion | flops 168689664 | bytes 986112 | tf_op jit(solution)/shard_map/while/body/eval_jaxpr/dot_general | solution.py:9
  90.5 0.4 fusion.34
  91.1 0.9 fusion.35
  92.0 1.6 %multiply_convert_fusion.6 = bf16[256,512]{1,0:T(8,128)(2,1)S(1)} fusion(bf16[1,512,512]{2,1,0:T(8,128)(2,1)} %get-tuple-element.400, f32[512]{0:T(512)S(1)} %bitcast.71, bf16[16,128,512]{2,1,0:T(8,128)(2,1)} %get-tuple-element.399, s32[]{:T(128)S(6)} %select_n.74, bf16[16,256,128]{2,1,0:T(8,128)(2,1)} %get-tuple-element.398), kind=kOutput, calls=%fused_computation.11.clone.1 | convolution fusion | flops 168689664 | bytes 986112 | tf_op jit(solution)/shard_map/while/body/eval_jaxpr/dot_general | solution.py:9
  93.7 0.4 fusion.34
  94.1 0.2 multiply_reduce_fusion.2
  94.3 0.9 fusion.35
  95.1 1.6 %multiply_convert_fusion.6 = bf16[256,512]{1,0:T(8,128)(2,1)S(1)} fusion(bf16[1,512,512]{2,1,0:T(8,128)(2,1)} %get-tuple-element.400, f32[512]{0:T(512)S(1)} %bitcast.71, bf16[16,128,512]{2,1,0:T(8,128)(2,1)} %get-tuple-element.399, s32[]{:T(128)S(6)} %select_n.74, bf16[16,256,128]{2,1,0:T(8,128)(2,1)} %get-tuple-element.398), kind=kOutput, calls=%fused_computation.11.clone.1 | convolution fusion | flops 168689664 | bytes 986112 | tf_op jit(solution)/shard_map/while/body/eval_jaxpr/dot_general | solution.py:9
  96.8 0.4 fusion.34
  97.4 0.9 fusion.35
  98.3 1.6 %multiply_convert_fusion.6 = bf16[256,512]{1,0:T(8,128)(2,1)S(1)} fusion(bf16[1,512,512]{2,1,0:T(8,128)(2,1)} %get-tuple-element.400, f32[512]{0:T(512)S(1)} %bitcast.71, bf16[16,128,512]{2,1,0:T(8,128)(2,1)} %get-tuple-element.399, s32[]{:T(128)S(6)} %select_n.74, bf16[16,256,128]{2,1,0:T(8,128)(2,1)} %get-tuple-element.398), kind=kOutput, calls=%fused_computation.11.clone.1 | convolution fusion | flops 168689664 | bytes 986112 | tf_op jit(solution)/shard_map/while/body/eval_jaxpr/dot_general | solution.py:9
  99.9 0.4 fusion.34
  100.6 0.9 fusion.35
  101.4 1.6 %multiply_convert_fusion.6 = bf16[256,512]{1,0:T(8,128)(2,1)S(1)} fusion(bf16[1,512,512]{2,1,0:T(8,128)(2,1)} %get-tuple-element.400, f32[512]{0:T(512)S(1)} %bitcast.71, bf16[16,128,512]{2,1,0:T(8,128)(2,1)} %get-tuple-element.399, s32[]{:T(128)S(6)} %select_n.74, bf16[16,256,128]{2,1,0:T(8,128)(2,1)} %get-tuple-element.398), kind=kOutput, calls=%fused_computation.11.clone.1 | convolution fusion | flops 168689664 | bytes 986112 | tf_op jit(solution)/shard_map/while/body/eval_jaxpr/dot_general | solution.py:9
  103.1 0.4 fusion.34
  103.7 0.9 fusion.35
  104.6 1.6 %multiply_convert_fusion.6 = bf16[256,512]{1,0:T(8,128)(2,1)S(1)} fusion(bf16[1,512,512]{2,1,0:T(8,128)(2,1)} %get-tuple-element.400, f32[512]{0:T(512)S(1)} %bitcast.71, bf16[16,128,512]{2,1,0:T(8,128)(2,1)} %get-tuple-element.399, s32[]{:T(128)S(6)} %select_n.74, bf16[16,256,128]{2,1,0:T(8,128)(2,1)} %get-tuple-element.398), kind=kOutput, calls=%fused_computation.11.clone.1 | convolution fusion | flops 168689664 | bytes 986112 | tf_op jit(solution)/shard_map/while/body/eval_jaxpr/dot_general | solution.py:9
  106.2 0.4 fusion.34
  106.8 0.9 fusion.35
  107.7 1.6 %multiply_convert_fusion.6 = bf16[256,512]{1,0:T(8,128)(2,1)S(1)} fusion(bf16[1,512,512]{2,1,0:T(8,128)(2,1)} %get-tuple-element.400, f32[512]{0:T(512)S(1)} %bitcast.71, bf16[16,128,512]{2,1,0:T(8,128)(2,1)} %get-tuple-element.399, s32[]{:T(128)S(6)} %select_n.74, bf16[16,256,128]{2,1,0:T(8,128)(2,1)} %get-tuple-element.398), kind=kOutput, calls=%fused_computation.11.clone.1 | convolution fusion | flops 168689664 | bytes 986112 | tf_op jit(solution)/shard_map/while/body/eval_jaxpr/dot_general | solution.py:9
  109.3 0.4 fusion.34
  110.0 0.9 fusion.35
  110.8 1.6 %multiply_convert_fusion.6 = bf16[256,512]{1,0:T(8,128)(2,1)S(1)} fusion(bf16[1,512,512]{2,1,0:T(8,128)(2,1)} %get-tuple-element.400, f32[512]{0:T(512)S(1)} %bitcast.71, bf16[16,128,512]{2,1,0:T(8,128)(2,1)} %get-tuple-element.399, s32[]{:T(128)S(6)} %select_n.74, bf16[16,256,128]{2,1,0:T(8,128)(2,1)} %get-tuple-element.398), kind=kOutput, calls=%fused_computation.11.clone.1 | convolution fusion | flops 168689664 | bytes 986112 | tf_op jit(solution)/shard_map/while/body/eval_jaxpr/dot_general | solution.py:9
  112.5 0.4 fusion.34
  113.1 0.9 fusion.35
  114.0 1.7 %multiply_convert_fusion.6 = bf16[256,512]{1,0:T(8,128)(2,1)S(1)} fusion(bf16[1,512,512]{2,1,0:T(8,128)(2,1)} %get-tuple-element.400, f32[512]{0:T(512)S(1)} %bitcast.71, bf16[16,128,512]{2,1,0:T(8,128)(2,1)} %get-tuple-element.399, s32[]{:T(128)S(6)} %select_n.74, bf16[16,256,128]{2,1,0:T(8,128)(2,1)} %get-tuple-element.398), kind=kOutput, calls=%fused_computation.11.clone.1 | convolution fusion | flops 168689664 | bytes 986112 | tf_op jit(solution)/shard_map/while/body/eval_jaxpr/dot_general | solution.py:9
  115.6 0.4 fusion.34
  116.2 0.9 fusion.35
  117.1 1.6 %multiply_convert_fusion.6 = bf16[256,512]{1,0:T(8,128)(2,1)S(1)} fusion(bf16[1,512,512]{2,1,0:T(8,128)(2,1)} %get-tuple-element.400, f32[512]{0:T(512)S(1)} %bitcast.71, bf16[16,128,512]{2,1,0:T(8,128)(2,1)} %get-tuple-element.399, s32[]{:T(128)S(6)} %select_n.74, bf16[16,256,128]{2,1,0:T(8,128)(2,1)} %get-tuple-element.398), kind=kOutput, calls=%fused_computation.11.clone.1 | convolution fusion | flops 168689664 | bytes 986112 | tf_op jit(solution)/shard_map/while/body/eval_jaxpr/dot_general | solution.py:9
  118.8 0.4 fusion.34
  119.4 0.9 fusion.35
  120.2 1.6 %multiply_convert_fusion.6 = bf16[256,512]{1,0:T(8,128)(2,1)S(1)} fusion(bf16[1,512,512]{2,1,0:T(8,128)(2,1)} %get-tuple-element.400, f32[512]{0:T(512)S(1)} %bitcast.71, bf16[16,128,512]{2,1,0:T(8,128)(2,1)} %get-tuple-element.399, s32[]{:T(128)S(6)} %select_n.74, bf16[16,256,128]{2,1,0:T(8,128)(2,1)} %get-tuple-element.398), kind=kOutput, calls=%fused_computation.11.clone.1 | convolution fusion | flops 168689664 | bytes 986112 | tf_op jit(solution)/shard_map/while/body/eval_jaxpr/dot_general | solution.py:9
  121.9 0.4 fusion.34
  122.5 0.9 fusion.35
  123.4 1.6 %multiply_convert_fusion.6 = bf16[256,512]{1,0:T(8,128)(2,1)S(1)} fusion(bf16[1,512,512]{2,1,0:T(8,128)(2,1)} %get-tuple-element.400, f32[512]{0:T(512)S(1)} %bitcast.71, bf16[16,128,512]{2,1,0:T(8,128)(2,1)} %get-tuple-element.399, s32[]{:T(128)S(6)} %select_n.74, bf16[16,256,128]{2,1,0:T(8,128)(2,1)} %get-tuple-element.398), kind=kOutput, calls=%fused_computation.11.clone.1 | convolution fusion | flops 168689664 | bytes 986112 | tf_op jit(solution)/shard_map/while/body/eval_jaxpr/dot_general | solution.py:9
  125.0 0.4 fusion.34
  125.4 0.2 multiply_reduce_fusion.2
  125.6 0.9 fusion.35
  126.5 9.4 %all_to_all.15 = f32[12,16,256]{2,0,1:T(8,128)S(1)} all-to-all(f32[12,16,256]{2,0,1:T(8,128)} %get-tuple-element.270), channel_id=1, replica_groups=mesh['band'=8,'patch'=4] {'patch'}, dimensions={1} | all-to-all | bytes 393216 | tf_op jit(solution)/shard_map/all_to_all | solution.py:67
  136.0 0.9 broadcast_in_dim_reshape.3
  (65 shorter events, 2.7 us)
Async XLA Ops:
  7.4 1.8 %copy-start = (bf16[1,2560,512]{2,1,0:T(8,128)(2,1)S(1)}, bf16[1,2560,512]{2,1,0:T(8,128)(2,1)}, u32[]{:S(2)}) copy-start(bf16[1,2560,512]{2,1,0:T(8,128)(2,1)} %param.13) | copy-start | bytes 7864324
  7.4 68.2 %all-reduce.2.cloned.1.call-start = ((), (), s32[]{:S(2)}) async-start(), calls=%async_computation.2 | async-start | bytes 4194304 | tf_op jit(solution)/shard_map/psum | solution.py:58
  9.1 9.2 %copy-start.7 = (s32[16]{0:T(128)S(1)}, s32[16]{0:T(128)}, u32[]{:S(2)}) copy-start(s32[16]{0:T(128)} %param.14) | copy-start | bytes 196
  21.2 55.1 %copy-start.1 = (bf16[1,512,512]{2,1,0:T(8,128)(2,1)S(1)}, bf16[1,512,512]{2,1,0:T(8,128)(2,1)}, u32[]{:S(2)}) copy-start(bf16[1,512,512]{2,1,0:T(8,128)(2,1)} %param.19) | copy-start | bytes 1572868
  21.2 55.1 %copy-start.2 = (bf16[1,12,512]{2,1,0:T(8,128)(2,1)S(1)}, bf16[1,12,512]{2,1,0:T(8,128)(2,1)}, u32[]{:S(2)}) copy-start(bf16[1,12,512]{2,1,0:T(8,128)(2,1)} %param.22) | copy-start | bytes 36868
  21.2 55.1 %copy-start.3 = (f32[1,512]{1,0:T(1,128)S(1)}, f32[1,512]{1,0:T(1,128)}, u32[]{:S(2)}) copy-start(f32[1,512]{1,0:T(1,128)} %param.20) | copy-start | bytes 6148
  21.2 55.1 %copy-start.4 = (f32[1,512]{1,0:T(1,128)S(1)}, f32[1,512]{1,0:T(1,128)}, u32[]{:S(2)}) copy-start(f32[1,512]{1,0:T(1,128)} %param.21) | copy-start | bytes 6148
  21.2 55.1 %copy-start.5 = (f32[1,12]{1,0:T(1,128)S(1)}, f32[1,12]{1,0:T(1,128)}, u32[]{:S(2)}) copy-start(f32[1,12]{1,0:T(1,128)} %param.23) | copy-start | bytes 148
  21.2 55.1 %copy-start.6 = (f32[1,512]{1,0:T(1,128)S(1)}, f32[1,512]{1,0:T(1,128)}, u32[]{:S(2)}) copy-start(f32[1,512]{1,0:T(1,128)} %param.18) | copy-start | bytes 6148
  21.3 54.3 %all-gather.2.cloned.1.call-start = ((), (), s32[]{:S(2)}) async-start(), calls=%async_computation.1 | async-start | bytes 1179648 | tf_op jit(solution)/shard_map/all_gather | solution.py:40
Sparse Core Ops, SparseCore 0:
  21.4 54.1 all-reduce.1
Sparse Core Ops, SparseCore 1:
  23.9 43.0 all-gather.1
where the time goes:
time: 145 us; the launch traced here: 144 us
  waiting for transfers between devices  54.2 us (37%)
  matrix products  46.4 us (32%)
  between operations  14.9 us (10%)
  local copies, waits for them, and re-layouts  11.2 us (8%)
  blocking collectives  9.38 us (6%)
  other arithmetic  7.95 us (5%)
    psum x1, waiting for transfers between devices, body(): all_blocks = lax.psum(filled.astype(jnp.bfloat16), 'patch')  53.7 us
    dot_general x16, matrix products, decode_rows(): jnp.dot(interp, w_first, preferred_element_type=jnp.float32) + b_first  26.3 us
    dot_general x16, matrix products, decode_rows(): lax.dot_general(w_out, normed, (((1,), (1,)), ((), ())), preferred_elemen...  13.9 us
    all_to_all x1, blocking collectives, body(): lax.all_to_all(decoded, 'patch', split_axis=1, concat_axis=2, tiled=True)  9.38 us
    gather x1, local copies, waits for them, and re-layouts, body(): jnp.take(local_latents, block_rows.reshape(-1), axis=0)  9.18 us
    dot_general x16, matrix products, decode_rows(): jnp.dot(hidden, w_second, preferred_element_type=jnp.float32) + b_second  6.16 us
    reduce_sum x16, other arithmetic, decode_rows(): variance = jnp.mean(centred * centred, axis=-1, keepdims=True)  3.28 us
    convert_element_type x1, other arithmetic, body(): all_blocks = lax.psum(filled.astype(jnp.bfloat16), 'patch')  2.9 us
  transfers between devices with their start and end apart: 2, of which 1 were waited for; matrix products, arithmetic and copies ran while one was open for 0% of the time, Pallas kernels for 0%

commit v1 on v0

--- a/solution.py
+++ b/solution.py
@@ -55,7 +55,7 @@
     )
     mine = (owners == my_index)[:, None, None]
     filled = jnp.where(mine, own_tiles.astype(jnp.float32), jnp.float32(0.0))
-    all_blocks = lax.psum(filled.astype(jnp.bfloat16), "patch")
+    all_blocks = jnp.sum(lax.all_gather(filled.astype(jnp.bfloat16), "patch"), axis=0)
 
     def visit_summed(turn_index, buffer):
         tile_index = turn_index % tile_count

time: 145 us -> 193 us (1.33)
  waiting for transfers between devices: 54.2 us -> 96.6 us
  other arithmetic: 7.95 us -> 14.9 us
    all_gather x0 -> x1, waiting for transfers between devices: none -> 60.3 us  [body(): lax.all_gather(filled.astype(jnp.bfloat16), 'patch')]
    psum x1 -> x0, waiting for transfers between devices: 53.7 us -> none  [body(): all_blocks = lax.psum(filled.astype(jnp.bfloat16), 'patch')]
    all_gather x1, waiting for transfers between devices: 0.01 us -> 35.5 us  [body(): weights_all = lax.all_gather(interp_weights, 'band', axis=0, tiled=True)]
    reduce_sum x0 -> x1, other arithmetic: none -> 6.9 us  [body(): jnp.sum(lax.all_gather(filled.astype(jnp.bfloat16), 'patch'), axis=0)]
  transfers between devices with their start and end apart: 2 -> 2, of which waited for: 1 -> 2; matrix products, arithmetic and copies ran while one was open for 0% -> 4% of each run, Pallas kernels for 0% -> 0%
where the time goes in v1:
time: 193 us; the launch traced here: 192 us
  waiting for transfers between devices  96.6 us (50%)
  matrix products  46.4 us (24%)
  other arithmetic  14.9 us (8%)
  between operations  13.5 us (7%)
  local copies, waits for them, and re-layouts  11.2 us (6%)
  blocking collectives  9.38 us (5%)
    all_gather x1, waiting for transfers between devices, body(): lax.all_gather(filled.astype(jnp.bfloat16), 'patch')  60.3 us
    all_gather x1, waiting for transfers between devices, body(): weights_all = lax.all_gather(interp_weights, 'band', axis=0, tiled=True)  35.5 us
    dot_general x16, matrix products, decode_rows(): jnp.dot(interp, w_first, preferred_element_type=jnp.float32) + b_first  26.4 us
    dot_general x16, matrix products, decode_rows(): lax.dot_general(w_out, normed, (((1,), (1,)), ((), ())), preferred_elemen...  13.9 us
    all_to_all x1, blocking collectives, body(): lax.all_to_all(decoded, 'patch', split_axis=1, concat_axis=2, tiled=True)  9.38 us
    gather x1, local copies, waits for them, and re-layouts, body(): jnp.take(local_latents, block_rows.reshape(-1), axis=0)  9.18 us
    reduce_sum x1, other arithmetic, body(): jnp.sum(lax.all_gather(filled.astype(jnp.bfloat16), 'patch'), axis=0)  6.9 us
    dot_general x16, matrix products, decode_rows(): jnp.dot(hidden, w_second, preferred_element_type=jnp.float32) + b_second  6.12 us
  transfers between devices with their start and end apart: 2, of which 2 were waited for; matrix products, arithmetic and copies ran while one was open for 4% of the time, Pallas kernels for 0%

profile of v1, /device:TPU:0, one launch (start us, length us, event | category | flops | bytes accessed | tf_op | source)
XLA Modules:
  0.0 192.2 jit_solution(4998509393439330468)
XLA Ops:
  6.5 0.9 compare_and_fusion
  7.4 0.7 compare_select_fusion
  8.3 9.2 %gather_fusion = bf16[2048,512]{1,0:T(8,128)(2,1)} fusion(bf16[2560,512]{1,0:T(8,128)(2,1)S(1)} %bitcast.62, s32[2048]{0:T(1024)S(1)} %broadcast_clamp_fusion), kind=kCustom, calls=%fused_computation | custom fusion | bytes 4202496 | tf_op jit(solution)/shard_map/jit(_take)/gather | solution.py:53
  17.5 2.9 %select_convert_fusion = bf16[1,16,128,512]{3,2,1,0:T(8,128)(2,1)} fusion(bf16[1,16,128,512]{3,2,1,0:T(8,128)(2,1)} %bitcast.63, pred[16]{0:T(512)(128)(4,1)S(1)} %broadcast_compare_fusion, pred[16,128]{1,0:T(8,128)(4,1)S(1)} %compare_and_fusion), kind=kLoop, calls=%fused_computation.23 | loop fusion | flops 4194304 | bytes 4196368 | tf_op jit(solution)/shard_map/convert_element_type | solution.py:58
  20.5 0.7 all-gather.3.cloned.1.call-update
  21.3 60.3 %all-gather.5.cloned.1.call-done = bf16[4,16,128,512]{3,2,1,0:T(8,128)(2,1)} async-done(((bf16[1,16,128,512]{3,2,1,0:T(8,128)(2,1)}), bf16[4,16,128,512]{3,2,1,0:T(8,128)(2,1)}) %all-gather.5.cloned.1.call-update) | async-done | bytes 8388624 | tf_op jit(solution)/shard_map/all_gather | solution.py:58
  81.6 6.9 %reduce_sum.44 = bf16[16,128,512]{2,1,0:T(8,128)(2,1)} reduce(bf16[4,16,128,512]{3,2,1,0:T(8,128)(2,1)} %all-gather.5.cloned.1.call-done, bf16[]{:T(256)} %constant.124.clone.1), dimensions={0}, to_apply=%region_0.1 | reduce | flops 3145728 | bytes 10485762 | tf_op jit(solution)/shard_map/reduce_sum | solution.py:58
  88.5 35.5 %all-gather.3.cloned.1.call-done = bf16[16,256,128]{2,1,0:T(8,128)(2,1)} async-done(((bf16[2,256,128]{2,1,0:T(8,128)(2,1)}), bf16[16,256,128]{2,1,0:T(8,128)(2,1)}) %all-gather.3.cloned.1.call-update) | async-done | bytes 1048592 | tf_op jit(solution)/shard_map/all_gather | solution.py:40
  124.0 0.7 broadcast_in_dim.43
  124.8 50.2 %while.15 = (s32[]{:T(128)}, f32[12,16,256]{2,0,1:T(8,128)}, bf16[16,256,128]{2,1,0:T(8,128)(2,1)}, bf16[16,128,512]{2,1,0:T(8,128)(2,1)}, bf16[1,512,512]{2,1,0...) while((s32[]{:T(128)}, f32[12,16,256]{2,0,1:T(8,128)}, ...), condition=%wide.region_4.5_spmd, body=%wide.region_1.4_spmd.sunk | while | flops 307236096 | bytes 3387677 | solution.py:66
  124.8 1.7 multiply_convert_fusion.6
  126.4 0.4 fusion.34
  126.8 0.2 multiply_reduce_fusion.2
  127.0 0.9 fusion.35
  127.9 1.6 multiply_convert_fusion.6
  129.6 0.4 fusion.34
  130.0 0.2 multiply_reduce_fusion.2
  130.2 0.9 fusion.35
  131.0 1.6 multiply_convert_fusion.6
  132.7 0.4 fusion.34
  133.1 0.2 multiply_reduce_fusion.2
  133.3 0.9 fusion.35
  134.2 1.6 multiply_convert_fusion.6
  135.8 0.4 fusion.34
  136.2 0.2 multiply_reduce_fusion.2
  136.4 0.9 fusion.35
  137.3 1.7 multiply_convert_fusion.6
  139.0 0.4 fusion.34
  139.6 0.9 fusion.35
  140.5 1.7 multiply_convert_fusion.6
  142.1 0.4 fusion.34
  142.7 0.9 fusion.35
  143.6 1.6 multiply_convert_fusion.6
  145.2 0.4 fusion.34
  145.9 0.9 fusion.35
  146.7 1.6 multiply_convert_fusion.6
  148.4 0.4 fusion.34
  149.0 0.9 fusion.35
  149.9 1.6 multiply_convert_fusion.6
  151.5 0.4 fusion.34
  152.1 0.9 fusion.35
  153.0 1.7 multiply_convert_fusion.6
  154.7 0.4 fusion.34
  155.3 0.9 fusion.35
  156.1 1.6 multiply_convert_fusion.6
  157.8 0.4 fusion.34
  158.4 0.9 fusion.35
  159.3 1.7 multiply_convert_fusion.6
  160.9 0.4 fusion.34
  161.5 0.9 fusion.35
  162.4 1.6 multiply_convert_fusion.6
  164.1 0.4 fusion.34
  164.7 0.9 fusion.35
  165.5 1.7 multiply_convert_fusion.6
  167.2 0.4 fusion.34
  167.8 0.9 fusion.35
  168.7 1.6 multiply_convert_fusion.6
  170.3 0.4 fusion.34
  170.9 0.9 fusion.35
  171.8 1.6 multiply_convert_fusion.6
  173.5 0.4 fusion.34
  174.1 0.9 fusion.35
  175.0 9.4 %all_to_all.15 = f32[12,16,256]{2,0,1:T(8,128)S(1)} all-to-all(f32[12,16,256]{2,0,1:T(8,128)} %get-tuple-element.270), channel_id=1, replica_groups=mesh['band'=8,'patch'=4] {'patch'}, dimensions={1} | all-to-all | bytes 393216 | tf_op jit(solution)/shard_map/all_to_all | solution.py:67
  184.5 0.9 broadcast_in_dim_reshape.3
  (66 shorter events, 3.1 us)
Async XLA Ops:
  6.5 1.8 copy-start
  6.5 75.0 %all-gather.5.cloned.1.call-start = ((), (), s32[]{:S(2)}) async-start(), calls=%async_computation.2 | async-start | bytes 10485760 | tf_op jit(solution)/shard_map/all_gather | solution.py:58
  8.3 9.2 %copy-start.7 = (s32[16]{0:T(128)S(1)}, s32[16]{0:T(128)}, u32[]{:S(2)}) copy-start(s32[16]{0:T(128)} %param.14) | copy-start | bytes 196
  20.4 103.6 %all-gather.3.cloned.1.call-start = ((), (), s32[]{:S(2)}) async-start(), calls=%async_computation.1 | async-start | bytes 1179648 | tf_op jit(solution)/shard_map/all_gather | solution.py:40
  21.2 103.5 %copy-start.1 = (bf16[1,512,512]{2,1,0:T(8,128)(2,1)S(1)}, bf16[1,512,512]{2,1,0:T(8,128)(2,1)}, u32[]{:S(2)}) copy-start(bf16[1,512,512]{2,1,0:T(8,128)(2,1)} %param.19) | copy-start | bytes 1572868
  21.2 103.5 %copy-start.2 = (bf16[1,12,512]{2,1,0:T(8,128)(2,1)S(1)}, bf16[1,12,512]{2,1,0:T(8,128)(2,1)}, u32[]{:S(2)}) copy-start(bf16[1,12,512]{2,1,0:T(8,128)(2,1)} %param.22) | copy-start | bytes 36868
  21.2 103.5 %copy-start.3 = (f32[1,512]{1,0:T(1,128)S(1)}, f32[1,512]{1,0:T(1,128)}, u32[]{:S(2)}) copy-start(f32[1,512]{1,0:T(1,128)} %param.20) | copy-start | bytes 6148
  21.2 103.5 %copy-start.4 = (f32[1,512]{1,0:T(1,128)S(1)}, f32[1,512]{1,0:T(1,128)}, u32[]{:S(2)}) copy-start(f32[1,512]{1,0:T(1,128)} %param.21) | copy-start | bytes 6148
  21.2 103.5 %copy-start.5 = (f32[1,12]{1,0:T(1,128)S(1)}, f32[1,12]{1,0:T(1,128)}, u32[]{:S(2)}) copy-start(f32[1,12]{1,0:T(1,128)} %param.23) | copy-start | bytes 148
  21.2 103.5 %copy-start.6 = (f32[1,512]{1,0:T(1,128)S(1)}, f32[1,512]{1,0:T(1,128)}, u32[]{:S(2)}) copy-start(f32[1,512]{1,0:T(1,128)} %param.18) | copy-start | bytes 6148
Sparse Core Ops, SparseCore 0:
  20.6 60.9 all-gather.4
  83.7 40.2 all-gather.2
